TPU v7x, 32 devices: a whole 2x2x4 slice. The times are simulated.
32 devices in a mesh: dp: 4 (over x, core), ctx: 8 (over z, y).
Axes of the slice: x: 2, y: 2, z: 4, core: 2. Of those that a mesh axis runs over, the one named last changes fastest.
Arguments:
- tokens: bfloat16 [4, 4096, 2048], P('dp', 'ctx'), may hold values from -6 to 6
- in_weight: bfloat16 [2048, 5120], P(None, 'dp'), may hold values from -0.125 to 0.125
- step_weight: bfloat16 [2048, 64], replicated, may hold values from -0.125 to 0.125
- step_bias: float32 [64], replicated, may hold values from -3 to 0
- decay_rate: float32 [64], replicated, may hold values from 0.0001 to 0.5
- skip_gain: float32 [64], replicated, may hold values from 0.5 to 1.5
- filter_taps: float32 [4, 5120], replicated, may hold values from -3 to 3
- filter_bias: float32 [5120], replicated, may hold values from -3 to 3
- norm_gain: float32 [4096], replicated, may hold values from 0.5 to 1.5
Outputs:
- normed: bfloat16 [4, 4096, 4096], P('dp', 'ctx')
All inputs are finite; a program needn't handle non-finite values.
Results may differ from a plain program's by a relative error of at most 0.0061.
Values may be sent and summed in bfloat16 or wider, within the bound.
A program may use at most 192 MiB of HBM per device.

v0:
```python
import math
import jax
import jax.numpy as jnp
from jax import lax
from jax.sharding import PartitionSpec as P

HEADS = 64
HEAD_DIM = 64
STATE = 128
GROUPS = 4
BLOCK = 256
GROUP_HEADS = 16


def shifted(value, axis, steps):
    count = lax.axis_size(axis)
    initial, last = (max(0, -steps), min(count, count - steps))
    return lax.ppermute(value, axis, [(source, source + steps) for source in range(initial, last)])


def filter_rows(prefix, current, filter_taps, filter_bias):
    padded = jnp.concatenate([prefix, current], axis=0).astype(jnp.float32)
    length = current.shape[0]
    summed = filter_bias + filter_taps[0] * padded[0:length]
    for offset in range(1, filter_taps.shape[0]):
        summed = summed + filter_taps[offset] * padded[offset : offset + length]
    return summed


def ssd_group(values, input_map, output_map, step_size, decay_rate, skip_gain, block_len):
    length, head_count, head_width = values.shape
    block_count = length // block_len
    bundle = math.gcd(block_count, 8)
    bundle_count = block_count // bundle
    highest = lax.Precision.HIGHEST
    value_rows = values.reshape(block_count, block_len, head_count, head_width)
    input_rows = input_map.reshape(block_count, block_len, -1)
    output_rows = output_map.reshape(block_count, block_len, -1)
    step_rows = step_size.reshape(block_count, block_len, head_count)
    decay_sum = jnp.cumsum(-step_rows * decay_rate, axis=1)
    causal = (jnp.arange(block_len)[:, None] >= jnp.arange(block_len)[None, :])[None, :, :, None]

    def local_block(pieces):
        value_block, input_block, output_block, step_block, decay_block = pieces
        scores = jnp.einsum(
            "ktn,kun->ktu", output_block, input_block, preferred_element_type=jnp.float32
        )
        decay_gap = jnp.where(causal, decay_block[:, :, None, :] - decay_block[:, None, :, :], 0.0)
        weights = (
            jnp.where(causal, jnp.exp(decay_gap), 0.0)
            * scores[..., None]
            * step_block[:, None, :, :]
        ).astype(jnp.bfloat16)
        within = jnp.einsum(
            "ktuh,kuhp->kthp", weights, value_block, preferred_element_type=jnp.float32
        )
        to_end = jnp.exp(decay_block[:, -1:, :] - decay_block) * step_block
        scaled = (to_end[..., None] * value_block.astype(jnp.float32)).astype(jnp.bfloat16)
        states = jnp.einsum(
            "kuhp,kun->khpn", scaled, input_block, preferred_element_type=jnp.float32
        )
        return (within, states)

    def blocked(array):
        return array.reshape((bundle_count, bundle) + array.shape[1:])

    within, states = lax.map(
        local_block,
        (
            blocked(value_rows),
            blocked(input_rows),
            blocked(output_rows),
            blocked(step_rows),
            blocked(decay_sum),
        ),
    )
    within = within.reshape(block_count, block_len, head_count, head_width)
    states = states.reshape((block_count,) + states.shape[2:])
    totals = decay_sum[:, -1, :]
    running = jnp.cumsum(totals, axis=0)
    starts = running - totals
    before = (jnp.arange(block_count)[:, None] > jnp.arange(block_count)[None, :])[:, :, None]
    mixing = jnp.where(
        before, jnp.exp(jnp.where(before, starts[:, None, :] - running[None, :, :], 0.0)), 0.0
    )
    entering = jnp.einsum("kjh,jhpn->khpn", mixing, states, precision=highest)
    carried = (
        jnp.einsum("khpn,ktn->kthp", entering, output_rows.astype(jnp.float32), precision=highest)
        * jnp.exp(decay_sum)[..., None]
    )
    output = within + carried + skip_gain[:, None] * value_rows.astype(jnp.float32)
    return output.reshape(length, head_count, head_width)


def group_norm(values, norm_gain):
    length = values.shape[0]
    grouped = values.astype(jnp.float32).reshape(length, GROUPS, -1)
    mean_square = jnp.mean(jnp.square(grouped), axis=-1, keepdims=True)
    return (grouped * lax.rsqrt(mean_square + 1e-05)).reshape(length, -1) * norm_gain


def sequence_filter(projected, filter_taps, filter_bias):
    reach_rows = filter_taps.shape[0] - 1
    length = projected.shape[0]
    rim_rows = shifted(projected[length - reach_rows :], "ctx", 1)
    return jax.nn.silu(filter_rows(rim_rows, projected, filter_taps, filter_bias)).astype(
        jnp.bfloat16
    )


def head_layout(source, step_raw, step_bias, decay_rate, skip_gain):
    context_size = lax.axis_size("ctx")
    device = lax.axis_index("ctx")
    length = source.shape[0]
    inner_width = HEADS * HEAD_DIM
    local_heads = HEADS // context_size
    local_width = local_heads * HEAD_DIM
    group_share = max(1, GROUP_HEADS // local_heads)
    local_groups = max(1, local_heads // GROUP_HEADS)
    value_parts = source[:, :inner_width].reshape(length, context_size, local_width)
    map_parts = source[:, inner_width:].reshape(length, 2, GROUPS, STATE)
    map_parts = jnp.repeat(map_parts, group_share, axis=2)
    step_parts = step_raw.reshape(length, context_size, local_heads)
    moved_values, moved_input, moved_output, moved_steps = (
        lax.all_to_all(value_parts, "ctx", split_axis=1, concat_axis=0, tiled=True),
        lax.all_to_all(map_parts[:, 0], "ctx", split_axis=1, concat_axis=0, tiled=True),
        lax.all_to_all(map_parts[:, 1], "ctx", split_axis=1, concat_axis=0, tiled=True),
        lax.all_to_all(step_parts, "ctx", split_axis=1, concat_axis=0, tiled=True),
    )
    full_length = moved_values.shape[0]
    head_values = moved_values.reshape(full_length, local_width)
    input_maps = moved_input.reshape(full_length, local_groups * STATE)
    output_maps = moved_output.reshape(full_length, local_groups * STATE)
    bias_slice = lax.dynamic_slice_in_dim(step_bias, device * local_heads, local_heads, 0)
    rate_slice = lax.dynamic_slice_in_dim(decay_rate, device * local_heads, local_heads, 0)
    skip_slice = lax.dynamic_slice_in_dim(skip_gain, device * local_heads, local_heads, 0)
    step_size = jax.nn.softplus(
        moved_steps.reshape(full_length, local_heads).astype(jnp.float32) + bias_slice
    )
    inputs = head_values.reshape(full_length, local_heads, HEAD_DIM)
    pieces = ssd_group(inputs, input_maps, output_maps, step_size, rate_slice, skip_slice, BLOCK)
    mixed_rows = pieces.reshape(full_length, local_width).astype(jnp.bfloat16)
    return lax.all_to_all(mixed_rows, "ctx", split_axis=0, concat_axis=1, tiled=True)


def per_device(
    tokens,
    in_weight,
    step_weight,
    step_bias,
    decay_rate,
    skip_gain,
    filter_taps,
    filter_bias,
    norm_gain,
):
    token_rows = tokens[0]
    projected = jnp.dot(
        token_rows,
        lax.all_gather(in_weight, "dp", axis=1, tiled=True),
        preferred_element_type=jnp.float32,
    ).astype(jnp.bfloat16)
    step_raw = jnp.dot(token_rows, step_weight, preferred_element_type=jnp.float32).astype(
        jnp.bfloat16
    )
    active = sequence_filter(projected, filter_taps, filter_bias)
    mixed_rows = head_layout(active, step_raw, step_bias, decay_rate, skip_gain)
    return group_norm(mixed_rows, norm_gain).astype(jnp.bfloat16)[None]


def solution(mesh):
    in_specs = (P("dp", "ctx", None), P(None, "dp"), P(), P(), P(), P(), P(), P(), P())
    out_specs = P("dp", "ctx", None)
    return jax.shard_map(
        per_device, mesh=mesh, in_specs=in_specs, out_specs=out_specs, check_vma=False
    )
```

profile of v0, /device:TPU:0, one launch (start us, length us, event | category | flops | bytes accessed | tf_op | source)
XLA Modules:
  0.0 554.3 jit_solution(2078704967498910302)
XLA Ops:
  10.5 7.3 %all-to-all-start.1 = ((bf16[512,8,8]{0,2,1:T(8,128)(2,1)}), bf16[512,8,8]{0,2,1:T(8,128)(2,1)S(1)}, u32[]{:S(2)}, u32[]{:S(2)}) async-start(bf16[512,8,8]{0,2,1:T(8,128)(2,1)} %fusion.45), calls=%async_computation.1 | async-start | bytes 131072 | tf_op jit(solution)/shard_map/all_to_all | solution.py:128
  17.8 125.4 %all-gather.2.cloned.1.call-done = bf16[2048,5120]{1,0:T(8,128)(2,1)} async-done(((bf16[2048,1280]{1,0:T(8,128)(2,1)}), bf16[2048,5120]{1,0:T(8,128)(2,1)}) %all-gather.2.cloned.1.call-update) | async-done | bytes 20971536 | tf_op jit(solution)/shard_map/all_gather | solution.py:160
  143.2 15.2 %convolution_convert_fusion = bf16[512,5120]{1,0:T(8,128)(2,1)S(1)} fusion(bf16[2048,5120]{1,0:T(8,128)(2,1)} %all-gather.2.cloned.1.call-done, bf16[1,512,2048]{2,1,0:T(8,128)(2,1)S(1)} %copy-done), kind=kOutput, calls=%fused_computation.49 | convolution fusion | flops 10740039680 | bytes 28311552 | tf_op jit(solution)/shard_map/dot_general | solution.py:158
  158.4 3.4 collective-permute-start
  165.0 6.7 %multiply_convert_fusion.8 = bf16[512,5120]{1,0:T(8,128)(2,1)S(1)} fusion(f32[515,5120]{1,0:T(8,128)S(1)} %maximum_convert_fusion, f32[5120]{0:T(1024)S(1)} %bitcast.192, f32[5120]{0:T(1024)S(1)} %bitcast.193, f32[5120]{0:T(1024)S(1)} %bitcast.191, f32[5120]{0:T(1024)S(1)} %bitcast.190, f32[5120]{0:T(1024)S(1)} %copy-done.7), kind=kLoop, calls=%fused_computation.40 | loop fusion | flops 34078720 | bytes 47288320 | tf_op jit(solution)/shard_map/convert_element_type | solution.py:106
  177.0 6.4 %all-to-all-start.2 = ((bf16[512,8,128]{2,0,1:T(8,128)(2,1)}), bf16[512,8,128]{2,0,1:T(8,128)(2,1)}, u32[]{:S(2)}, u32[]{:S(2)}) async-start(bf16[512,8,128]{2,0,1:T(8,128)(2,1)} %get-tuple-element.173), calls=%async_computation.2 | async-start | bytes 2097152 | tf_op jit(solution)/shard_map/all_to_all | solution.py:127
  183.4 4.7 slice.75
  188.1 6.5 %copy.167 = bf16[512,4096]{0,1:T(8,128)(2,1)} copy(bf16[512,4096]{1,0:T(8,128)(2,1)} %slice.75) | data formatting | bytes 8388608 | tf_op jit(solution)/shard_map/reshape | solution.py:120
  194.6 14.2 %all-to-all-done.2 = bf16[512,8,128]{2,0,1:T(8,128)(2,1)} async-done(((bf16[512,8,128]{2,0,1:T(8,128)(2,1)}), bf16[512,8,128]{2,0,1:T(8,128)(2,1)}, u32[]{:S(2)}, u32[]{:S(2)}) %all-to-all-start.2) | async-done | bytes 1048608 | tf_op jit(solution)/shard_map/all_to_all | solution.py:127
  208.8 4.6 all-to-all-start
  214.2 91.4 %all-to-all-done = bf16[512,8,512]{0,2,1:T(8,128)(2,1)} async-done(((bf16[512,8,512]{0,2,1:T(8,128)(2,1)}), bf16[512,8,512]{0,2,1:T(8,128)(2,1)}, u32[]{:S(2)}, u32[]{:S(2)}) %all-to-all-start) | async-done | bytes 4194336 | tf_op jit(solution)/shard_map/all_to_all | solution.py:125
  305.6 4.7 all-to-all-start.3
  310.5 9.0 %reduce-window.6 = f32[16,8,2,128]{3,1,2,0:T(8,128)S(1)} reduce-window(f32[16,8,2,128]{3,1,2,0:T(8,128)S(1)} %fusion.50, f32[]{:T(128)} %constant.30.clone.1), window={size=1x1x1x128 pad=0_0x0_0x0_0x127_0}, to_apply=%region_0.1 | reduce-window | flops 4161536 | bytes 262148 | tf_op jit(solution)/shard_map/reduce-window
  321.5 6.5 %copy.143 = bf16[8,512,1,512]{1,0,3,2:T(8,128)(2,1)} copy(bf16[8,512,1,512]{1,3,0,2:T(8,128)(2,1)} %bitcast.7) | data formatting | bytes 8388608 | tf_op jit(solution)/shard_map/all_to_all | solution.py:125
  327.9 7.1 %reshape_reshape_reshape_reshape.3 = bf16[2,8,256,8,64]{2,1,0,4,3:T(8,128)(2,1)} reshape(bf16[8,512,1,512]{1,0,3,2:T(8,128)(2,1)} %copy.143) | data formatting | bytes 8388608 | tf_op jit(solution)/shard_map/reshape;reshape;reshape;reshape | solution.py:65
  335.9 34.5 %while.14 = (s32[]{:T(128)}, f32[2,8,256,8,64]{2,4,3,1,0:T(8,128)}, f32[2,8,8,64,128]{4,3,2,1,0:T(8,128)}, bf16[2,8,256,8,64]{2,1,0,4,3:T(8,128)(2,1)}, f32[2,8,...) while((s32[]{:T(128)}, f32[2,8,256,8,64]{2,4,3,1,0:T(8,128)}, ...), condition=%wide.region_3.4_spmd.clone.clone, body=%wide.region_2.3_spmd.clone.clone.sunk | while | flops 967933952 | bytes 30084480 | solution.py:67
  340.6 7.4 %bitcast_dynamic-update-slice_fusion.4 = f32[2,8,256,8,64]{2,4,3,1,0:T(8,128)} fusion(f32[2,8,256,8,64]{2,4,3,1,0:T(8,128)} %get-tuple-element.241, s32[]{:T(128)} %get-tuple-element.240, f32[8,256,8]{1,2,0:T(8,128)S(1)} %bitcast.182, f32[8,256,256]{2,1,0:T(8,128)S(1)} %fusion.77, f32[8,256,8]{1,2,0:T(8,128)S(1)} %bitcast.183, ...), kind=kOutput, calls=%fused_computation.9.clone.1 | convolution fusion | flops 562036736 | bytes 8651264 | tf_op jit(solution)/shard_map/while/body/eval_jaxpr/ktuh,kuhp->kthp/dot_general | solution.py:54
  349.4 3.7 bitcast_dynamic-update-slice_fusion.5
  357.9 7.4 %bitcast_dynamic-update-slice_fusion.4 = f32[2,8,256,8,64]{2,4,3,1,0:T(8,128)} fusion(f32[2,8,256,8,64]{2,4,3,1,0:T(8,128)} %get-tuple-element.241, s32[]{:T(128)} %get-tuple-element.240, f32[8,256,8]{1,2,0:T(8,128)S(1)} %bitcast.182, f32[8,256,256]{2,1,0:T(8,128)S(1)} %fusion.77, f32[8,256,8]{1,2,0:T(8,128)S(1)} %bitcast.183, ...), kind=kOutput, calls=%fused_computation.9.clone.1 | convolution fusion | flops 562036736 | bytes 8651264 | tf_op jit(solution)/shard_map/while/body/eval_jaxpr/ktuh,kuhp->kthp/dot_general | solution.py:54
  366.7 3.7 bitcast_dynamic-update-slice_fusion.5
  370.4 3.4 bitcast_convert_fusion.1
  373.8 8.1 %copy.158 = f32[8,512,1,512]{1,0,3,2:T(8,128)} copy(f32[8,512,1,512]{1,3,0,2:T(8,128)S(1)} %bitcast_convert_fusion.1) | data formatting | bytes 16777216 | tf_op jit(solution)/shard_map/convert_element_type | solution.py:91
  381.8 9.5 %reshape.194 = f32[16,256,8,64]{1,0,3,2:T(8,128)} reshape(f32[8,512,1,512]{1,0,3,2:T(8,128)} %copy.158) | data formatting | bytes 16777216 | tf_op jit(solution)/shard_map/convert_element_type | solution.py:91
  391.3 10.2 %fusion.36 = f32[16,8,64,128]{3,0,2,1:T(8,128)} fusion(f32[16,8,64,128]{3,2,1,0:T(8,128)} %bitcast.186, f32[16,8]{0,1:T(8,128)S(1)} %copy.153, f32[16,8]{0,1:T(8,128)S(1)} %fusion.62, pred[16,16]{1,0:T(8,128)(4,1)S(1)} %iota_compare_fusion.1), kind=kOutput, calls=%fused_computation.55 | convolution fusion | flops 201332736 | bytes 8389888 | tf_op jit(solution)/shard_map/kjh,jhpn->khpn/dot_general | solution.py:86
  401.6 15.8 %fusion.29 = bf16[16,256,8,64]{1,3,2,0:T(8,128)(2,1)} fusion(f32[2,8,256,8,64]{2,4,3,1,0:T(8,128)} %get-tuple-element.56, f32[16,256,8,64]{1,0,3,2:T(8,128)S(1)} %copy-done.4, f32[8]{0:T(128)S(1)} %copy-done.9, f32[16,256,8]{1,2,0:T(8,128)S(1)} %copy.157, bf16[16,256,128,1]{2,1,3,0:T(8,128)(2,1)} %bitcast.34, f32[16,8,64,128]{3,0,2,1:T(8,128)} %fusion.36), kind=kOutput, calls=%fused_computation.46 | convolution fusion | flops 3231711232 | bytes 26345504 | tf_op jit(solution)/shard_map/khpn,ktn->kthp/dot_general | solution.py:88
  417.4 6.7 %copy.160 = bf16[16,256,8,64]{1,0,3,2:T(8,128)(2,1)} copy(bf16[16,256,8,64]{1,3,2,0:T(8,128)(2,1)} %fusion.29) | data formatting | bytes 8388608 | tf_op jit(solution)/shard_map/convert_element_type | solution.py:142
  424.1 7.1 %convert_element_type.101 = bf16[8,512,512]{1,0,2:T(8,128)(2,1)} reshape(bf16[16,256,8,64]{1,0,3,2:T(8,128)(2,1)} %copy.160) | data formatting | bytes 8388608 | tf_op jit(solution)/shard_map/convert_element_type | solution.py:142
  431.2 3.6 copy.161
  434.8 97.4 %all_to_all.64 = bf16[8,512,512]{1,2,0:T(8,128)(2,1)S(1)} all-to-all(bf16[8,512,512]{1,2,0:T(8,128)(2,1)S(1)} %copy.161), channel_id=1, replica_groups=mesh['dp'=4,'ctx'=8] {'ctx'}, dimensions={0} | all-to-all | bytes 8388608 | tf_op jit(solution)/shard_map/all_to_all | solution.py:143
  535.1 3.3 convert_element_type.116
  538.5 2.4 fusion.27
  540.9 6.3 %copy.163 = bf16[1,512,4096]{2,1,0:T(8,128)(2,1)} copy(bf16[1,512,4096]{1,2,0:T(8,128)(2,1)} %fusion.27) | data formatting | bytes 8388608 | tf_op jit(solution)/shard_map/convert_element_type | solution.py:168
  (88 shorter events, 31.1 us)
Async XLA Ops:
  6.5 1.6 copy-start
  6.5 136.7 %all-gather.2.cloned.1.call-start = ((), (), s32[]{:S(2)}) async-start(), calls=%async_computation.5 | async-start | bytes 26214400 | tf_op jit(solution)/shard_map/all_gather | solution.py:160
  10.5 166.6 %all-to-all-start.1 = ((bf16[512,8,8]{0,2,1:T(8,128)(2,1)}), bf16[512,8,8]{0,2,1:T(8,128)(2,1)S(1)}, u32[]{:S(2)}, u32[]{:S(2)}) async-start(bf16[512,8,8]{0,2,1:T(8,128)(2,1)} %fusion.45), calls=%async_computation.1 | async-start | bytes 131072 | tf_op jit(solution)/shard_map/all_to_all | solution.py:128
  17.8 144.0 %copy-start.6 = (f32[4,5120]{1,0:T(4,128)S(1)}, f32[4,5120]{1,0:T(4,128)}, u32[]{:S(2)}) copy-start(f32[4,5120]{1,0:T(4,128)} %param.17) | copy-start | bytes 245764
  158.4 6.6 %copy-start.7 = (f32[5120]{0:T(1024)S(1)}, f32[5120]{0:T(1024)}, u32[]{:S(2)}) copy-start(f32[5120]{0:T(1024)} %param.18) | copy-start | bytes 61444
  158.4 5.0 collective-permute-start
  171.8 2.3 copy-start.5
  177.0 31.7 %all-to-all-start.2 = ((bf16[512,8,128]{2,0,1:T(8,128)(2,1)}), bf16[512,8,128]{2,0,1:T(8,128)(2,1)}, u32[]{:S(2)}, u32[]{:S(2)}) async-start(bf16[512,8,128]{2,0,1:T(8,128)(2,1)} %get-tuple-element.173), calls=%async_computation.2 | async-start | bytes 2097152 | tf_op jit(solution)/shard_map/all_to_all | solution.py:127
  188.1 25.3 %copy-start.10 = (f32[64]{0:T(128)S(1)}, f32[64]{0:T(128)}, u32[]{:S(2)}) copy-start(f32[64]{0:T(128)} %param.14) | copy-start | bytes 772
  188.1 25.4 %copy-start.11 = (f32[64]{0:T(128)S(1)}, f32[64]{0:T(128)}, u32[]{:S(2)}) copy-start(f32[64]{0:T(128)} %param.15) | copy-start | bytes 772
  188.1 25.4 %copy-start.12 = (f32[64]{0:T(128)S(1)}, f32[64]{0:T(128)}, u32[]{:S(2)}) copy-start(f32[64]{0:T(128)} %param.16) | copy-start | bytes 772
  208.8 96.8 %all-to-all-start = ((bf16[512,8,512]{0,2,1:T(8,128)(2,1)}), bf16[512,8,512]{0,2,1:T(8,128)(2,1)}, u32[]{:S(2)}, u32[]{:S(2)}) async-start(bf16[512,8,512]{0,2,1:T(8,128)(2,1)} %bitcast.180), calls=%async_computation | async-start | bytes 8388608 | tf_op jit(solution)/shard_map/all_to_all | solution.py:125
  305.6 30.3 %all-to-all-start.3 = ((bf16[512,8,128]{2,0,1:T(8,128)(2,1)}), bf16[512,8,128]{2,0,1:T(8,128)(2,1)}, u32[]{:S(2)}, u32[]{:S(2)}) async-start(bf16[512,8,128]{2,0,1:T(8,128)(2,1)} %get-tuple-element.172), calls=%async_computation.3 | async-start | bytes 2097152 | tf_op jit(solution)/shard_map/all_to_all | solution.py:126
  339.3 1.3 copy-start.2
  356.5 1.3 copy-start.2
  391.3 10.3 %copy-start.4 = (f32[16,256,8,64]{1,0,3,2:T(8,128)S(1)}, f32[16,256,8,64]{1,0,3,2:T(8,128)}, u32[]{:S(2)}) copy-start(f32[16,256,8,64]{1,0,3,2:T(8,128)} %reshape.194) | copy-start | bytes 25165828
  391.3 10.3 %copy-start.9 = (f32[8]{0:T(128)S(1)}, f32[8]{0:T(128)}, u32[]{:S(2)}) copy-start(f32[8]{0:T(128)} %dynamic_slice.29) | copy-start | bytes 100
  532.2 2.0 copy-start.3
  534.2 4.3 copy-start.8
  538.5 8.8 %copy-start.1 = (bf16[1,512,2048]{2,1,0:T(8,128)(2,1)S(1)}, bf16[1,512,2048]{2,1,0:T(8,128)(2,1)}, u32[]{:S(2)}) copy-start(bf16[1,512,2048]{2,1,0:T(8,128)(2,1)} %param.11) | copy-start | bytes 6291460
Sparse Core Ops, SparseCore 0:
  8.9 134.2 all-gather.1
where the time goes:
time: 563 us; the launch traced here: 554 us
  waiting for transfers between devices  234 us (42%)
  blocking collectives  97.4 us (17%)
  local copies, waits for them, and re-layouts  84.9 us (15%)
  matrix products  69.2 us (12%)
  other arithmetic  28.3 us (5%)
  starting transfers between devices  26.3 us (5%)
  between operations  14 us (2%)
    all_gather x1, waiting for transfers between devices, per_device(): lax.all_gather(in_weight, 'dp', axis=1, tiled=True)  125 us
    all_to_all x1, blocking collectives, head_layout(): lax.all_to_all(mixed_rows, 'ctx', split_axis=0, concat_axis=1, tiled=True)  97.4 us
    all_to_all x1, waiting for transfers between devices, head_layout(): lax.all_to_all(value_parts, 'ctx', split_axis=1, concat_axis=0, tiled=True)  91.4 us
    convert_element_type x2, local copies, waits for them, and re-layouts, ssd_group(): value_rows.astype(jnp.float32)  17.6 us
    convert_element_type x3, local copies, waits for them, and re-layouts, head_layout(): mixed_rows = pieces.reshape(full_length, local_width).astype(jnp.bfloat16)  17.4 us
    dot_general x1, matrix products, ssd_group(): jnp.einsum('khpn,ktn->kthp', entering, output_rows.astype(jnp.float32), p...  15.8 us
    dot_general x1, matrix products, per_device(): jnp.dot(token_rows, lax.all_gather(in_weight, 'dp', axis=1, tiled=True),...  15.2 us
    dot_general x2, matrix products, local_block(): jnp.einsum('ktuh,kuhp->kthp', weights, value_block, preferred_element_typ...  14.9 us
  transfers between devices with their start and end apart: 6, of which 5 were waited for; matrix products, arithmetic and copies ran while one was open for 12% of the time, Pallas kernels for 0%

commit v1 on v0

--- a/solution.py
+++ b/solution.py
@@ -10,6 +10,12 @@
 GROUPS = 4
 BLOCK = 256
 GROUP_HEADS = 16
+
+
+def gathered_along(array, axis, d):
+    pieces = lax.all_gather(array, axis, axis=0, tiled=False)
+    full = jnp.concatenate(pieces, axis=d)
+    return full
 
 
 def shifted(value, axis, steps):
@@ -156,9 +162,7 @@
 ):
     token_rows = tokens[0]
     projected = jnp.dot(
-        token_rows,
-        lax.all_gather(in_weight, "dp", axis=1, tiled=True),
-        preferred_element_type=jnp.float32,
+        token_rows, gathered_along(in_weight, "dp", 1), preferred_element_type=jnp.float32
     ).astype(jnp.bfloat16)
     step_raw = jnp.dot(token_rows, step_weight, preferred_element_type=jnp.float32).astype(
         jnp.bfloat16

time: 563 us -> 584 us (1.037)
  local copies, waits for them, and re-layouts: 84.9 us -> 111 us
  waiting for transfers between devices: 234 us -> 224 us
    reshape x0 -> x1, local copies, waits for them, and re-layouts: none -> 27.2 us  [gathered_along(): full = jnp.concatenate(pieces, axis=d)]
    all_to_all x1, waiting for transfers between devices: 14.2 us -> 0.01 us  [head_layout(): lax.all_to_all(map_parts[:, 1], 'ctx', split_axis=1, concat_axis=0, tiled...]
    all_to_all x1, waiting for transfers between devices: 0.86 us -> 14.1 us  [head_layout(): lax.all_to_all(map_parts[:, 0], 'ctx', split_axis=1, concat_axis=0, tiled...]
    all_to_all x1, waiting for transfers between devices: 91.4 us -> 82.4 us  [head_layout(): lax.all_to_all(value_parts, 'ctx', split_axis=1, concat_axis=0, tiled=True)]
  transfers between devices with their start and end apart: 6 -> 6, of which waited for: 5 -> 4; matrix products, arithmetic and copies ran while one was open for 12% -> 21% of each run, Pallas kernels for 0% -> 0%
where the time goes in v1:
time: 584 us; the launch traced here: 574 us
  waiting for transfers between devices  224 us (38%)
  local copies, waits for them, and re-layouts  111 us (19%)
  blocking collectives  98.3 us (17%)
  matrix products  69.6 us (12%)
  other arithmetic  30.7 us (5%)
  starting transfers between devices  26 us (4%)
  between operations  14.1 us (2%)
    all_gather x1, waiting for transfers between devices, gathered_along(): pieces = lax.all_gather(array, axis, axis=0, tiled=False)  125 us
    all_to_all x1, blocking collectives, head_layout(): lax.all_to_all(mixed_rows, 'ctx', split_axis=0, concat_axis=1, tiled=True)  98.3 us
    all_to_all x1, waiting for transfers between devices, head_layout(): lax.all_to_all(value_parts, 'ctx', split_axis=1, concat_axis=0, tiled=True)  82.4 us
    reshape x1, local copies, waits for them, and re-layouts, gathered_along(): full = jnp.concatenate(pieces, axis=d)  27.2 us
    convert_element_type x2, local copies, waits for them, and re-layouts, ssd_group(): value_rows.astype(jnp.float32)  17.4 us
    convert_element_type x3, local copies, waits for them, and re-layouts, head_layout(): mixed_rows = pieces.reshape(full_length, local_width).astype(jnp.bfloat16)  17.4 us
    dot_general x1, matrix products, per_device(): jnp.dot(token_rows, gathered_along(in_weight, 'dp', 1), preferred_element...  16.8 us
    dot_general x1, matrix products, ssd_group(): jnp.einsum('khpn,ktn->kthp', entering, output_rows.astype(jnp.float32), p...  15.9 us
  transfers between devices with their start and end apart: 6, of which 4 were waited for; matrix products, arithmetic and copies ran while one was open for 21% of the time, Pallas kernels for 0%

profile of v1, /device:TPU:0, one launch (start us, length us, event | category | flops | bytes accessed | tf_op | source)
XLA Modules:
  0.0 574.0 jit_solution(10332112448981647271)
XLA Ops:
  10.5 7.3 %all-to-all-start.1 = ((bf16[512,8,8]{0,2,1:T(8,128)(2,1)}), bf16[512,8,8]{0,2,1:T(8,128)(2,1)S(1)}, u32[]{:S(2)}, u32[]{:S(2)}) async-start(bf16[512,8,8]{0,2,1:T(8,128)(2,1)} %fusion.45), calls=%async_computation.1 | async-start | bytes 131072 | tf_op jit(solution)/shard_map/all_to_all | solution.py:134
  17.8 125.5 %all-gather.3.cloned.1.call-done = bf16[8192,1280]{1,0:T(8,128)(2,1)} async-done(((bf16[2048,1280]{1,0:T(8,128)(2,1)}), bf16[8192,1280]{1,0:T(8,128)(2,1)}) %all-gather.3.cloned.1.call-update) | async-done | bytes 20971536 | tf_op jit(solution)/shard_map/all_gather | solution.py:16
  143.2 27.2 %copy.146 = bf16[2048,4,1280]{0,2,1:T(8,128)(2,1)} copy(bf16[2048,4,1280]{2,0,1:T(8,128)(2,1)} %bitcast.184) | data formatting | bytes 41943040 | tf_op jit(solution)/shard_map/reshape | solution.py:17
  170.4 16.8 %convolution_convert_fusion = bf16[512,5120]{1,0:T(8,128)(2,1)} fusion(bf16[2048,5120]{0,1:T(8,128)(2,1)} %bitcast.185, bf16[1,512,2048]{2,1,0:T(8,128)(2,1)S(1)} %copy-done), kind=kOutput, calls=%fused_computation.49 | convolution fusion | flops 10740039680 | bytes 28311552 | tf_op jit(solution)/shard_map/dot_general | solution.py:164
  188.1 3.4 collective-permute-start
  193.1 4.0 maximum_convert_fusion
  197.2 6.7 %multiply_convert_fusion.8 = bf16[512,5120]{1,0:T(8,128)(2,1)S(1)} fusion(f32[515,5120]{1,0:T(8,128)S(1)} %maximum_convert_fusion, f32[5120]{0:T(1024)S(1)} %bitcast.198, f32[5120]{0:T(1024)S(1)} %bitcast.199, f32[5120]{0:T(1024)S(1)} %bitcast.197, f32[5120]{0:T(1024)S(1)} %bitcast.196, f32[5120]{0:T(1024)S(1)} %copy-done.8), kind=kLoop, calls=%fused_computation.40 | loop fusion | flops 34078720 | bytes 47288320 | tf_op jit(solution)/shard_map/convert_element_type | solution.py:112
  209.1 6.4 %all-to-all-start.3 = ((bf16[512,8,128]{2,0,1:T(8,128)(2,1)}), bf16[512,8,128]{2,0,1:T(8,128)(2,1)}, u32[]{:S(2)}, u32[]{:S(2)}) async-start(bf16[512,8,128]{2,0,1:T(8,128)(2,1)} %get-tuple-element.172), calls=%async_computation.3 | async-start | bytes 2097152 | tf_op jit(solution)/shard_map/all_to_all | solution.py:132
  215.5 4.7 slice.75
  220.2 6.5 %copy.172 = bf16[512,4096]{0,1:T(8,128)(2,1)} copy(bf16[512,4096]{1,0:T(8,128)(2,1)} %slice.75) | data formatting | bytes 8388608 | tf_op jit(solution)/shard_map/reshape | solution.py:126
  226.7 14.1 %all-to-all-done.3 = bf16[512,8,128]{2,0,1:T(8,128)(2,1)} async-done(((bf16[512,8,128]{2,0,1:T(8,128)(2,1)}), bf16[512,8,128]{2,0,1:T(8,128)(2,1)}, u32[]{:S(2)}, u32[]{:S(2)}) %all-to-all-start.3) | async-done | bytes 1048608 | tf_op jit(solution)/shard_map/all_to_all | solution.py:132
  240.8 4.5 all-to-all-start
  245.8 9.0 %reduce-window.6 = f32[16,8,2,128]{3,1,2,0:T(8,128)S(1)} reduce-window(f32[16,8,2,128]{3,1,2,0:T(8,128)S(1)} %fusion.50, f32[]{:T(128)} %constant.30.clone.1), window={size=1x1x1x128 pad=0_0x0_0x0_0x127_0}, to_apply=%region_0.1 | reduce-window | flops 4161536 | bytes 262148 | tf_op jit(solution)/shard_map/reduce-window
  255.3 82.4 %all-to-all-done = bf16[512,8,512]{0,2,1:T(8,128)(2,1)} async-done(((bf16[512,8,512]{0,2,1:T(8,128)(2,1)}), bf16[512,8,512]{0,2,1:T(8,128)(2,1)}, u32[]{:S(2)}, u32[]{:S(2)}) %all-to-all-start) | async-done | bytes 4194336 | tf_op jit(solution)/shard_map/all_to_all | solution.py:131
  337.7 4.4 all-to-all-start.2
  344.2 6.5 %copy.148 = bf16[8,512,1,512]{1,0,3,2:T(8,128)(2,1)} copy(bf16[8,512,1,512]{1,3,0,2:T(8,128)(2,1)} %bitcast.10) | data formatting | bytes 8388608 | tf_op jit(solution)/shard_map/all_to_all | solution.py:131
  350.7 7.1 %reshape_reshape_reshape_reshape.3 = bf16[2,8,256,8,64]{2,1,0,4,3:T(8,128)(2,1)} reshape(bf16[8,512,1,512]{1,0,3,2:T(8,128)(2,1)} %copy.148) | data formatting | bytes 8388608 | tf_op jit(solution)/shard_map/reshape;reshape;reshape;reshape | solution.py:71
  357.8 3.4 bitcast_convert_fusion.1
  361.2 8.1 %copy.163 = f32[8,512,1,512]{1,0,3,2:T(8,128)} copy(f32[8,512,1,512]{1,3,0,2:T(8,128)S(1)} %bitcast_convert_fusion.1) | data formatting | bytes 16777216 | tf_op jit(solution)/shard_map/convert_element_type | solution.py:97
  369.3 9.3 %reshape.202 = f32[16,256,8,64]{1,0,3,2:T(8,128)} reshape(f32[8,512,1,512]{1,0,3,2:T(8,128)} %copy.163) | data formatting | bytes 16777216 | tf_op jit(solution)/shard_map/convert_element_type | solution.py:97
  378.6 31.3 %while.14 = (s32[]{:T(128)}, f32[2,8,256,8,64]{2,4,3,1,0:T(8,128)}, f32[2,8,8,64,128]{4,3,2,1,0:T(8,128)}, bf16[2,8,256,8,64]{2,1,0,4,3:T(8,128)(2,1)}, f32[2,8,...) while((s32[]{:T(128)}, f32[2,8,256,8,64]{2,4,3,1,0:T(8,128)}, ...), condition=%wide.region_3.4_spmd.clone.clone, body=%wide.region_2.3_spmd.clone.clone.sunk | while | flops 967933952 | bytes 22743976 | solution.py:73
  383.6 3.1 bitcast_dynamic-update-slice_fusion.5
  386.7 7.5 %bitcast_dynamic-update-slice_fusion.4 = f32[2,8,256,8,64]{2,4,3,1,0:T(8,128)} fusion(f32[2,8,256,8,64]{2,4,3,1,0:T(8,128)} %get-tuple-element.241, s32[]{:T(128)S(6)} %copy.213, f32[8,256,8]{1,2,0:T(8,128)S(1)} %bitcast.188, f32[8,256,256]{2,1,0:T(8,128)S(1)} %fusion.77, f32[8,256,8]{1,2,0:T(8,128)S(1)} %bitcast.189, ...), kind=kOutput, calls=%fused_computation.9.clone.1 | convolution fusion | flops 562036736 | bytes 8650756 | tf_op jit(solution)/shard_map/while/body/eval_jaxpr/ktuh,kuhp->kthp/dot_general | solution.py:60
  402.2 7.5 %bitcast_dynamic-update-slice_fusion.4 = f32[2,8,256,8,64]{2,4,3,1,0:T(8,128)} fusion(f32[2,8,256,8,64]{2,4,3,1,0:T(8,128)} %get-tuple-element.241, s32[]{:T(128)S(6)} %copy.213, f32[8,256,8]{1,2,0:T(8,128)S(1)} %bitcast.188, f32[8,256,256]{2,1,0:T(8,128)S(1)} %fusion.77, f32[8,256,8]{1,2,0:T(8,128)S(1)} %bitcast.189, ...), kind=kOutput, calls=%fused_computation.9.clone.1 | convolution fusion | flops 562036736 | bytes 8650756 | tf_op jit(solution)/shard_map/while/body/eval_jaxpr/ktuh,kuhp->kthp/dot_general | solution.py:60
  409.9 10.2 %fusion.36 = f32[16,8,64,128]{3,0,2,1:T(8,128)} fusion(f32[16,8,64,128]{3,2,1,0:T(8,128)} %bitcast.192, f32[16,8]{0,1:T(8,128)S(1)} %copy.158, f32[16,8]{0,1:T(8,128)S(1)} %fusion.62, pred[16,16]{1,0:T(8,128)(4,1)S(1)} %iota_compare_fusion.1), kind=kOutput, calls=%fused_computation.55 | convolution fusion | flops 201332736 | bytes 8389888 | tf_op jit(solution)/shard_map/kjh,jhpn->khpn/dot_general | solution.py:92
  420.2 15.9 %fusion.29 = bf16[16,256,8,64]{1,3,2,0:T(8,128)(2,1)} fusion(f32[2,8,256,8,64]{2,4,3,1,0:T(8,128)} %get-tuple-element.56, f32[16,256,8,64]{1,0,3,2:T(8,128)S(1)} %copy-done.3, f32[8]{0:T(128)S(1)} %dynamic_slice.29, f32[16,256,8]{1,2,0:T(8,128)} %copy.162, bf16[16,256,128,1]{2,1,3,0:T(8,128)(2,1)} %bitcast.37, f32[16,8,64,128]{3,0,2,1:T(8,128)} %fusion.36), kind=kOutput, calls=%fused_computation.46 | convolution fusion | flops 3231711232 | bytes 26345504 | tf_op jit(solution)/shard_map/khpn,ktn->kthp/dot_general | solution.py:94
  436.0 6.7 %copy.165 = bf16[16,256,8,64]{1,0,3,2:T(8,128)(2,1)} copy(bf16[16,256,8,64]{1,3,2,0:T(8,128)(2,1)} %fusion.29) | data formatting | bytes 8388608 | tf_op jit(solution)/shard_map/convert_element_type | solution.py:148
  442.7 7.1 %convert_element_type.101 = bf16[8,512,512]{1,0,2:T(8,128)(2,1)} reshape(bf16[16,256,8,64]{1,0,3,2:T(8,128)(2,1)} %copy.165) | data formatting | bytes 8388608 | tf_op jit(solution)/shard_map/convert_element_type | solution.py:148
  449.8 3.6 copy.166
  453.4 98.3 %all_to_all.64 = bf16[8,512,512]{1,2,0:T(8,128)(2,1)S(1)} all-to-all(bf16[8,512,512]{1,2,0:T(8,128)(2,1)S(1)} %copy.166), channel_id=1, replica_groups=mesh['dp'=4,'ctx'=8] {'ctx'}, dimensions={0} | all-to-all | bytes 8388608 | tf_op jit(solution)/shard_map/all_to_all | solution.py:149
  554.6 3.3 convert_element_type.116
  560.4 6.3 %copy.168 = bf16[1,512,4096]{2,1,0:T(8,128)(2,1)} copy(bf16[1,512,4096]{1,2,0:T(8,128)(2,1)} %fusion.27) | data formatting | bytes 8388608 | tf_op jit(solution)/shard_map/convert_element_type | solution.py:172
  (91 shorter events, 32.9 us)
Async XLA Ops:
  6.5 1.6 copy-start
  6.5 136.7 %all-gather.3.cloned.1.call-start = ((), (), s32[]{:S(2)}) async-start(), calls=%async_computation.5 | async-start | bytes 26214400 | tf_op jit(solution)/shard_map/all_gather | solution.py:16
  10.5 198.6 %all-to-all-start.1 = ((bf16[512,8,8]{0,2,1:T(8,128)(2,1)}), bf16[512,8,8]{0,2,1:T(8,128)(2,1)S(1)}, u32[]{:S(2)}, u32[]{:S(2)}) async-start(bf16[512,8,8]{0,2,1:T(8,128)(2,1)} %fusion.45), calls=%async_computation.1 | async-start | bytes 131072 | tf_op jit(solution)/shard_map/all_to_all | solution.py:134
  170.4 21.1 %copy-start.7 = (f32[4,5120]{1,0:T(4,128)S(1)}, f32[4,5120]{1,0:T(4,128)}, u32[]{:S(2)}) copy-start(f32[4,5120]{1,0:T(4,128)} %param.17) | copy-start | bytes 245764
  187.2 10.0 %copy-start.8 = (f32[5120]{0:T(1024)S(1)}, f32[5120]{0:T(1024)}, u32[]{:S(2)}) copy-start(f32[5120]{0:T(1024)} %param.18) | copy-start | bytes 61444
  188.1 5.0 collective-permute-start
  203.9 2.3 copy-start.4
  209.1 31.7 %all-to-all-start.3 = ((bf16[512,8,128]{2,0,1:T(8,128)(2,1)}), bf16[512,8,128]{2,0,1:T(8,128)(2,1)}, u32[]{:S(2)}, u32[]{:S(2)}) async-start(bf16[512,8,128]{2,0,1:T(8,128)(2,1)} %get-tuple-element.172), calls=%async_computation.3 | async-start | bytes 2097152 | tf_op jit(solution)/shard_map/all_to_all | solution.py:132
  220.2 25.2 %copy-start.10 = (f32[64]{0:T(128)S(1)}, f32[64]{0:T(128)}, u32[]{:S(2)}) copy-start(f32[64]{0:T(128)} %param.14) | copy-start | bytes 772
  220.2 25.3 %copy-start.11 = (f32[64]{0:T(128)S(1)}, f32[64]{0:T(128)}, u32[]{:S(2)}) copy-start(f32[64]{0:T(128)} %param.15) | copy-start | bytes 772
  220.2 25.4 %copy-start.12 = (f32[64]{0:T(128)S(1)}, f32[64]{0:T(128)}, u32[]{:S(2)}) copy-start(f32[64]{0:T(128)} %param.16) | copy-start | bytes 772
  240.8 96.8 %all-to-all-start = ((bf16[512,8,512]{0,2,1:T(8,128)(2,1)}), bf16[512,8,512]{0,2,1:T(8,128)(2,1)}, u32[]{:S(2)}, u32[]{:S(2)}) async-start(bf16[512,8,512]{0,2,1:T(8,128)(2,1)} %bitcast.186), calls=%async_computation | async-start | bytes 8388608 | tf_op jit(solution)/shard_map/all_to_all | solution.py:131
  337.7 41.0 %all-to-all-start.2 = ((bf16[512,8,128]{2,0,1:T(8,128)(2,1)}), bf16[512,8,128]{2,0,1:T(8,128)(2,1)}, u32[]{:S(2)}, u32[]{:S(2)}) async-start(bf16[512,8,128]{2,0,1:T(8,128)(2,1)} %get-tuple-element.173), calls=%async_computation.2 | async-start | bytes 2097152 | tf_op jit(solution)/shard_map/all_to_all | solution.py:133
  378.6 0.7 copy-start.5
  386.7 7.5 %copy-start.6 = (f32[2,8,256,8]{2,3,1,0:T(8,128)S(1)}, f32[2,8,256,8]{2,3,1,0:T(8,128)}, u32[]{:S(2)}) copy-start(f32[2,8,256,8]{2,3,1,0:T(8,128)} %copy-done.5) | copy-start | bytes 393220 | tf_op jit(solution)/shard_map/while
  394.2 0.6 copy-start.5
  402.2 7.5 %copy-start.6 = (f32[2,8,256,8]{2,3,1,0:T(8,128)S(1)}, f32[2,8,256,8]{2,3,1,0:T(8,128)}, u32[]{:S(2)}) copy-start(f32[2,8,256,8]{2,3,1,0:T(8,128)} %copy-done.5) | copy-start | bytes 393220 | tf_op jit(solution)/shard_map/while
  409.9 10.3 %copy-start.3 = (f32[16,256,8,64]{1,0,3,2:T(8,128)S(1)}, f32[16,256,8,64]{1,0,3,2:T(8,128)}, u32[]{:S(2)}) copy-start(f32[16,256,8,64]{1,0,3,2:T(8,128)} %reshape.202) | copy-start | bytes 25165828
  551.7 2.0 copy-start.2
  553.7 4.3 copy-start.9
  557.9 8.8 %copy-start.1 = (bf16[1,512,2048]{2,1,0:T(8,128)(2,1)S(1)}, bf16[1,512,2048]{2,1,0:T(8,128)(2,1)}, u32[]{:S(2)}) copy-start(bf16[1,512,2048]{2,1,0:T(8,128)(2,1)} %param.11) | copy-start | bytes 6291460
Sparse Core Ops, SparseCore 0:
  8.9 134.2 all-gather.2
